TPU v7x, 32 devices: a whole 2x2x4 slice. The times are simulated.
32 devices in a mesh: dom: 16 (over z, y, x), tm: 2 (over core).
Axes of the slice: x: 2, y: 2, z: 4, core: 2. Of those that a mesh axis runs over, the one named last changes fastest.
Arguments:
- sources: bfloat16 [256, 3, 16, 256], P('dom', None, 'tm'), may hold values from -6 to 6
- weights: bfloat16 [48, 16, 256, 256], P('dom', None, None, 'tm'), may hold values from -0.09375 to 0.09375
- intersect: int32 [48, 16], replicated, may hold values from 0 to 255, as said below
- block_row: int32 [256], replicated, may hold values from 0 to 255, as said below
- slot_tile: int32 [48], replicated, may hold values from 0 to 47, as said below
Outputs:
- acoustic_source: bfloat16 [48, 3, 16, 256], P('dom', None, 'tm')
- source_rate: bfloat16 [48, 3, 16, 256], P('dom', None, 'tm')
Inputs may be any that keep to these rules, and one draw needn't show every extreme that they name: `intersect`: over the 48 links of the slots held by one index of dom, exactly 24 distinct source rows are named, each by exactly two links; no index of dom holds more than 2 of these rows, and some index holds exactly 2. `block_row`: A permutation of the block ids. `slot_tile`: A permutation of the tile ids.
All inputs are finite; a program needn't handle non-finite values.
Results may differ from a plain program's by a relative error of at most 0.007.
Values may be sent and summed in bfloat16 or wider, within the bound.
A program may use at most 64 MiB of HBM per device.

v0:
```python
import jax
import jax.numpy as jnp
from jax import lax
from jax.sharding import PartitionSpec as P


def with_halo(cells, sides, width):
    for axis, dim in sides:
        count = lax.axis_size(axis)
        ends = count - 1
        head = lax.slice_in_dim(cells, 0, width, axis=dim)
        tail = lax.slice_in_dim(cells, cells.shape[dim] - width, cells.shape[dim], axis=dim)
        cells = jnp.concatenate(
            [
                lax.ppermute(tail, axis, [(i, (i + 1) % count) for i in range(ends)]),
                cells,
                lax.ppermute(head, axis, [((i + 1) % count, i) for i in range(ends)]),
            ],
            axis=dim,
        )
    return cells


def interpolate(received, link_index, used_weights):
    slot_total = received.shape[0] * received.shape[1]
    flattened = received.reshape((slot_total,) + received.shape[2:])
    picked = jnp.take(flattened, link_index, axis=0)
    tile_count = used_weights.shape[0]
    link_count = used_weights.shape[1]
    picked = picked.reshape(
        tile_count, link_count, picked.shape[1] * picked.shape[2], picked.shape[3]
    )
    combined = jnp.einsum(
        "tkrc,tkcn->trn", picked, used_weights, preferred_element_type=jnp.float32
    )
    return combined.reshape(tile_count, received.shape[2], received.shape[3], used_weights.shape[3])


def shards(sources, weights, intersect, block_row, slot_tile):
    domain_count = lax.axis_size("dom")
    my_index = lax.axis_index("dom")
    block_count = sources.shape[0]
    tile_count = weights.shape[0]
    link_count = tile_count * weights.shape[1]
    pool_size = link_count // 2
    per_owner = (pool_size + domain_count - 1) // domain_count
    all_rows = jnp.take(block_row, jnp.take(intersect, slot_tile, axis=0), axis=0)
    all_rows = all_rows.reshape(domain_count, link_count)
    all_owner = all_rows // block_count
    all_local = all_rows % block_count
    own_rows = lax.dynamic_index_in_dim(all_rows, my_index, 0, keepdims=False)
    own_owner = own_rows // block_count
    owned_here = all_owner == my_index
    row_range = jnp.arange(block_count)
    present = jnp.any(
        owned_here[:, :, None] & (all_local[:, :, None] == row_range[None, None, :]), axis=1
    )
    ranked = jnp.cumsum(present.astype(jnp.int32), axis=1) - 1
    wanted = present[:, :, None] & (ranked[:, :, None] == jnp.arange(per_owner)[None, None, :])
    send_index = jnp.max(jnp.where(wanted, row_range[None, :, None], -1), axis=1)
    global_range = jnp.arange(domain_count * block_count)
    needed = jnp.any(own_rows[:, None] == global_range[None, :], axis=0)
    needed_rank = (
        jnp.cumsum(needed.astype(jnp.int32).reshape(domain_count, block_count), axis=1) - 1
    )
    own_slot = jnp.take(needed_rank.reshape(-1), own_rows)
    link_index = own_owner * per_owner + own_slot
    used_weights = lax.all_gather(weights, "tm", axis=3, tiled=True)
    occupied = send_index >= 0
    packed = jnp.take(sources, jnp.maximum(send_index, 0).reshape(-1), axis=0)
    packed = packed.reshape((domain_count, per_owner) + sources.shape[1:])
    packed = jnp.where(occupied[:, :, None, None, None], packed, jnp.zeros((), packed.dtype))
    result = interpolate(
        lax.all_to_all(packed, "dom", split_axis=0, concat_axis=0, tiled=True),
        link_index,
        used_weights,
    )
    time_index = lax.axis_index("tm")
    time_count = lax.axis_size("tm")
    extended = with_halo(result.astype(jnp.bfloat16), (("tm", 2),), 1).astype(result.dtype)
    central = (extended[:, :, 2:] - extended[:, :, :-2]) * 0.5
    samples = result.shape[2]
    position = jnp.arange(samples)
    first_edge = result[:, :, 1:2] - result[:, :, 0:1]
    last_edge = result[:, :, -1:] - result[:, :, -2:-1]
    at_start = (position == 0) & (time_index == 0)
    at_end = (position == samples - 1) & (time_index == time_count - 1)
    derivative = jnp.where(at_start[None, None, :, None], first_edge, central)
    derivative = jnp.where(at_end[None, None, :, None], last_edge, derivative)
    return (result.astype(jnp.bfloat16), derivative.astype(jnp.bfloat16))


def solution(mesh):
    return jax.shard_map(
        shards,
        mesh=mesh,
        in_specs=(P("dom", None, "tm", None), P("dom", None, None, "tm"), P(), P(), P()),
        out_specs=(P("dom", None, "tm", None), P("dom", None, "tm", None)),
        check_vma=False,
    )
```

profile of v0, /device:TPU:0, one launch (start us, length us, event | category | flops | bytes accessed | tf_op | source)
XLA Modules:
  0.0 56.2 jit_solution(10402883597060521565)
XLA Ops:
  7.2 0.7 %all-gather.2.cloned.1.call-update = ((bf16[3,16,256,128]{3,2,1,0:T(8,128)(2,1)}), bf16[3,16,256,256]{3,2,1,0:T(8,128)(2,1)}) async-update(((), (), s32[]{:S(2)}) %all-gather.2.cloned.1.call-start, bf16[3,16,256,128]{3,2,1,0:T(8,128)(2,1)} %param.6) | async-update | bytes 12582936
  7.9 0.8 %copy.9 = s32[48,16]{1,0:T(8,128)S(1)} copy(s32[48,16]{0,1:T(8,128)} %param.7) | data formatting | bytes 6144 | tf_op args[2]
  8.7 0.7 %compare_select_fusion.4 = s32[48]{0:T(128)S(1)} fusion(s32[48]{0:T(128)} %param.9), kind=kLoop, calls=%fused_computation.55 | loop fusion | flops 144 | bytes 384 | tf_op jit(solution)/shard_map/jit(_take)/jit(_where)/select_n | solution.py:47
  9.4 0.6 %gather_fusion = s32[48,16]{1,0:T(8,128)S(1)} fusion(s32[48,16]{1,0:T(8,128)S(1)} %copy.9, s32[1024]{0:T(1024)S(1)} %pad_clamp_fusion.4), kind=kCustom, calls=%fused_computation | custom fusion | bytes 6336 | tf_op jit(solution)/shard_map/jit(_take)/gather | solution.py:47
  10.0 0.7 %compare_and_fusion.3 = pred[48]{0:T(512)(128)(4,1)S(1)} fusion(s32[48]{0:T(128)} %param.9), kind=kLoop, calls=%fused_computation.66 | loop fusion | flops 288 | bytes 240 | tf_op jit(solution)/shard_map/jit(_take)/and | solution.py:47
  10.7 0.1 broadcast_in_dim.118
  11.0 5.0 %gather_fusion.1 = s32[768]{0:T(1024)S(1)} fusion(s32[256]{0:T(256)S(1)} %copy-done.1, s32[1024]{0:T(1024)S(1)} %pad_clamp_fusion.3), kind=kCustom, calls=%fused_computation.1 | custom fusion | bytes 9216 | tf_op jit(solution)/shard_map/jit(_take)/gather | solution.py:47
  16.1 0.1 broadcast_in_dim.120
  16.3 0.4 fusion.4
  16.6 0.2 reduce_window_sum.18
  16.8 0.1 select_reduce_fusion
  16.9 0.1 copy.10
  17.0 0.1 copy.11
  17.1 0.1 copy.12
  17.2 0.1 reshape.368
  17.3 0.6 %gather_fusion.3 = bf16[32,3,8,256]{3,2,1,0:T(8,128)(2,1)S(1)} fusion(bf16[16,3,8,256]{3,2,1,0:T(8,128)(2,1)S(1)} %copy-done, s32[1024]{0:T(1024)S(1)} %pad_clamp_fusion.1), kind=kCustom, calls=%fused_computation.3 | custom fusion | bytes 786560 | tf_op jit(solution)/shard_map/jit(_take)/gather | solution.py:70
  17.9 0.9 %select_select_fusion = bf16[16,2,3,8,256]{4,3,2,1,0:T(8,128)(2,1)} fusion(bf16[16,2,3,8,256]{4,3,2,1,0:T(8,128)(2,1)S(1)} %bitcast.47, pred[16,2]{1,0:T(8,128)(4,1)S(1)} %copy.11, pred[16,2]{1,0:T(8,128)(4,1)S(1)} %copy.10), kind=kLoop, calls=%fused_computation.8 | loop fusion | flops 393216 | bytes 786496 | tf_op jit(solution)/shard_map/jit(_where)/select_n | solution.py:72
  18.8 8.3 %all-to-all-start = ((bf16[16,2,3,8,256]{4,3,2,1,0:T(8,128)(2,1)}), bf16[16,2,3,8,256]{4,3,2,1,0:T(8,128)(2,1)S(1)}, u32[]{:S(2)}, u32[]{:S(2)}) async-start(bf16[16,2,3,8,256]{4,3,2,1,0:T(8,128)(2,1)} %select_select_fusion), calls=%async_computation | async-start | bytes 786432 | tf_op jit(solution)/shard_map/all_to_all | solution.py:74
  27.2 0.5 broadcast.460
  27.7 0.7 %fusion.22 = (s32[48]{0:T(128)S(1)}, s32[1,48]{1,0:T(1,128)S(1)}) fusion(s32[]{:T(128)} %broadcast.460, s32[16,48]{1,0:T(8,128)S(1)} %get-tuple-element.5, s32[]{:T(128)S(6)} %select_n.195), kind=kLoop, calls=%fused_computation.80 | loop fusion | bytes 584 | tf_op jit(solution)/shard_map/jit(dynamic_index_in_dim)/dynamic_slice | solution.py:51
  28.4 0.1 fusion.9
  28.5 0.2 reduce_window_sum.17
  28.7 0.1 sub.33
  28.8 0.8 %gather_fusion.2 = s32[48]{0:T(128)S(1)} fusion(s32[256]{0:T(256)S(1)} %sub.33, s32[1024]{0:T(1024)S(1)} %pad_clamp_fusion.2), kind=kCustom, calls=%fused_computation.2 | custom fusion | bytes 576 | tf_op jit(solution)/shard_map/jit(_take)/gather | solution.py:66
  29.6 0.1 gather.40
  29.8 10.0 %all-to-all-done = bf16[16,2,3,8,256]{4,3,2,1,0:T(8,128)(2,1)S(1)} async-done(((bf16[16,2,3,8,256]{4,3,2,1,0:T(8,128)(2,1)}), bf16[16,2,3,8,256]{4,3,2,1,0:T(8,128)(2,1)S(1)}, u32[]{:S(2)}, u32[]{:S(2)}) %all-to-all-start) | async-done | bytes 393248 | tf_op jit(solution)/shard_map/all_to_all | solution.py:74
  39.8 0.6 %gather_fusion.4 = bf16[48,3,8,256]{3,2,1,0:T(8,128)(2,1)S(1)} fusion(bf16[32,3,8,256]{3,2,1,0:T(8,128)(2,1)S(1)} %bitcast.45, s32[1024]{0:T(1024)S(1)} %pad_clamp_fusion), kind=kCustom, calls=%fused_computation.4 | custom fusion | bytes 1179840 | tf_op jit(solution)/shard_map/jit(_take)/gather | solution.py:27
  40.4 3.8 %fusion.24 = (bf16[3,3,8,256]{3,2,1,0:T(8,128)(2,1)S(1)}, f32[3,3,8,256]{3,2,1,0:T(8,128)S(1)}) fusion(bf16[3,16,256,256]{3,2,1,0:T(8,128)(2,1)} %all-gather.2.cloned.1.call-done, bf16[3,16,24,256]{3,2,1,0:T(8,128)(2,1)S(1)} %bitcast.46, pred[3,16]{1,0:T(4,128)(4,1)S(1)} %compare_and_fusion.2), kind=kOutput, calls=%fused_computation.82 | convolution fusion | flops 151308288 | bytes 6991920 | tf_op jit(solution)/shard_map/tkrc,tkcn->trn/dot_general | solution.py:33
  44.3 1.3 %collective-permute-start = (bf16[3,3,1,256]{3,2,1,0:T(2,128)(2,1)S(1)}, bf16[3,3,1,256]{3,2,1,0:T(2,128)(2,1)S(1)}, u32[]{:S(2)}, u32[]{:S(2)}) collective-permute-start(bf16[3,3,1,256]{3,2,1,0:T(2,128)(2,1)S(1)} %get-tuple-element.8), channel_id=1, source_target_pairs={{0,1},{2,3},{4,5},{6,7},{8,9},{10,11},{12,13},{14,15},{16,17},{18,... | collective-permute-start | bytes 13832 | tf_op jit(solution)/shard_map/ppermute | solution.py:15
  45.6 1.3 %collective-permute-start.1 = (bf16[3,3,1,256]{3,2,1,0:T(2,128)(2,1)S(1)}, bf16[3,3,1,256]{3,2,1,0:T(2,128)(2,1)S(1)}, u32[]{:S(2)}, u32[]{:S(2)}) collective-permute-start(bf16[3,3,1,256]{3,2,1,0:T(2,128)(2,1)S(1)} %get-tuple-element.9), channel_id=1, source_target_pairs={{1,0},{3,2},{5,4},{7,6},{9,8},{11,10},{13,12},{15,14},{17,16},{19,... | collective-permute-start | bytes 13832 | tf_op jit(solution)/shard_map/ppermute | solution.py:17
  46.9 1.7 %collective-permute-done.1 = bf16[3,3,1,256]{3,2,1,0:T(2,128)(2,1)S(1)} collective-permute-done((bf16[3,3,1,256]{3,2,1,0:T(2,128)(2,1)S(1)}, bf16[3,3,1,256]{3,2,1,0:T(2,128)(2,1)S(1)}, u32[]{:S(2)}, u32[]{:S(2)}) %collective-permute-start.1) | collective-permute-done | bytes 4640 | tf_op jit(solution)/shard_map/ppermute | solution.py:17
  48.7 0.7 %fusion.8 = bf16[3,3,8,256]{3,2,1,0:T(8,128)(2,1)} fusion(f32[3,3,10,256]{3,2,1,0:T(8,128)S(1)} %maximum_convert_fusion, bf16[3,3,256]{2,1,0:T(4,128)(2,1)S(1)} %get-tuple-element.14, bf16[3,3,256]{2,1,0:T(4,128)(2,1)S(1)} %get-tuple-element.15, pred[8]{0:T(512)(128)(4,1)S(1)} %get-tuple-element.16, pred[8]{0:T(512)(128)(4,1)S(1)} %get-tuple-element.17), kind=kLoop, calls=%fused_computation.17 | loop fusion | flops 73728 | bytes 193552 | tf_op jit(solution)/shard_map/convert_element_type | solution.py:90
  (37 shorter events, 0.9 us)
Async XLA Ops:
  7.2 10.2 %copy-start = (bf16[16,3,8,256]{3,2,1,0:T(8,128)(2,1)S(1)}, bf16[16,3,8,256]{3,2,1,0:T(8,128)(2,1)}, u32[]{:S(2)}) copy-start(bf16[16,3,8,256]{3,2,1,0:T(8,128)(2,1)} %param.5) | copy-start | bytes 589828
  7.2 3.8 %copy-start.1 = (s32[256]{0:T(256)S(1)}, s32[256]{0:T(256)}, u32[]{:S(2)}) copy-start(s32[256]{0:T(256)} %param.8) | copy-start | bytes 3076
  7.2 33.2 %all-gather.2.cloned.1.call-start = ((), (), s32[]{:S(2)}) async-start(), calls=%async_computation.1 | async-start | bytes 9437184 | tf_op jit(solution)/shard_map/all_gather | solution.py:68
  18.8 21.0 %all-to-all-start = ((bf16[16,2,3,8,256]{4,3,2,1,0:T(8,128)(2,1)}), bf16[16,2,3,8,256]{4,3,2,1,0:T(8,128)(2,1)S(1)}, u32[]{:S(2)}, u32[]{:S(2)}) async-start(bf16[16,2,3,8,256]{4,3,2,1,0:T(8,128)(2,1)} %select_select_fusion), calls=%async_computation | async-start | bytes 786432 | tf_op jit(solution)/shard_map/all_to_all | solution.py:74
  44.2 5.2 %copy-start.2 = (bf16[3,3,8,256]{3,2,1,0:T(8,128)(2,1)}, bf16[3,3,8,256]{3,2,1,0:T(8,128)(2,1)S(1)}, u32[]{:S(2)}) copy-start(bf16[3,3,8,256]{3,2,1,0:T(8,128)(2,1)S(1)} %get-tuple-element.12) | copy-start | bytes 110596
  44.3 2.6 %collective-permute-start = (bf16[3,3,1,256]{3,2,1,0:T(2,128)(2,1)S(1)}, bf16[3,3,1,256]{3,2,1,0:T(2,128)(2,1)S(1)}, u32[]{:S(2)}, u32[]{:S(2)}) collective-permute-start(bf16[3,3,1,256]{3,2,1,0:T(2,128)(2,1)S(1)} %get-tuple-element.8), channel_id=1, source_target_pairs={{0,1},{2,3},{4,5},{6,7},{8,9},{10,11},{12,13},{14,15},{16,17},{18,... | collective-permute-start | bytes 13832 | tf_op jit(solution)/shard_map/ppermute | solution.py:15
  45.6 3.1 %collective-permute-start.1 = (bf16[3,3,1,256]{3,2,1,0:T(2,128)(2,1)S(1)}, bf16[3,3,1,256]{3,2,1,0:T(2,128)(2,1)S(1)}, u32[]{:S(2)}, u32[]{:S(2)}) collective-permute-start(bf16[3,3,1,256]{3,2,1,0:T(2,128)(2,1)S(1)} %get-tuple-element.9), channel_id=1, source_target_pairs={{1,0},{3,2},{5,4},{7,6},{9,8},{11,10},{13,12},{15,14},{17,16},{19,... | collective-permute-start | bytes 13832 | tf_op jit(solution)/shard_map/ppermute | solution.py:17
Sparse Core Ops, SparseCore 0:
  9.5 18.1 all-gather.1
where the time goes:
time: 56.6 us; the launch traced here: 56.2 us
  between operations  14.3 us (25%)
  waiting for transfers between devices  12.4 us (22%)
  starting transfers between devices  11 us (19%)
  local copies, waits for them, and re-layouts  10.7 us (19%)
  other arithmetic  4.11 us (7%)
  matrix products  3.78 us (7%)
    all_to_all x1, waiting for transfers between devices, shards(): lax.all_to_all(packed, 'dom', split_axis=0, concat_axis=0, tiled=True)  9.96 us
    all_to_all x1, starting transfers between devices, shards(): lax.all_to_all(packed, 'dom', split_axis=0, concat_axis=0, tiled=True)  8.34 us
    gather x2, local copies, waits for them, and re-layouts, shards(): jnp.take(block_row, jnp.take(intersect, slot_tile, axis=0), axis=0)  5.06 us
    dot_general x1, matrix products, interpolate(): jnp.einsum('tkrc,tkcn->trn', picked, used_weights, preferred_element_type...  3.78 us
    ppermute x1, waiting for transfers between devices, with_halo(): lax.ppermute(head, axis, [((i + 1) % count, i) for i in range(ends)])  1.74 us
    ppermute x1, starting transfers between devices, with_halo(): lax.ppermute(head, axis, [((i + 1) % count, i) for i in range(ends)])  1.29 us
    ppermute x1, starting transfers between devices, with_halo(): lax.ppermute(tail, axis, [(i, (i + 1) % count) for i in range(ends)])  1.29 us
    dynamic_slice x2, local copies, waits for them, and re-layouts, shards(): own_rows = lax.dynamic_index_in_dim(all_rows, my_index, 0, keepdims=False)  1.18 us
  transfers between devices with their start and end apart: 4, of which 2 were waited for; matrix products, arithmetic and copies ran while one was open for 25% of the time, Pallas kernels for 0%

commit v1 on v0

v1 whole, which is shorter than its diff:
```python
import functools

import jax
import jax.numpy as jnp
from jax import lax
from jax.experimental import pallas as pl
from jax.experimental.pallas import tpu as pltpu
from jax.sharding import PartitionSpec as P


def tables(sources, weights, intersect, block_row, slot_tile, per_owner, domains):
    me = lax.axis_index("dom")
    blocks = sources.shape[0]
    links = weights.shape[0] * weights.shape[1]
    tile_ids = jnp.arange(intersect.shape[0], dtype=jnp.int32)
    named = jnp.sum(
        jnp.where(slot_tile[:, None, None] == tile_ids[None, :, None], intersect[None], 0), axis=1
    )
    named = named.reshape(domains, links)
    block_ids = jnp.arange(block_row.shape[0], dtype=jnp.int32)
    rows = jnp.sum(jnp.where(named[:, :, None] == block_ids, block_row, 0), axis=2)
    first = me * blocks
    local = rows - first
    mine = (local >= 0) & (local < blocks)
    picks = []
    last = jnp.full((domains, 1), -1, jnp.int32)
    for _ in range(per_owner):
        ahead = jnp.where(mine & (local > last), local, blocks - 1)
        last = jnp.min(ahead, axis=1, keepdims=True)
        picks.append(last)
    send = jnp.concatenate(picks, axis=1).reshape(-1)
    own = lax.dynamic_index_in_dim(rows, me, 0, keepdims=False)
    owner = own // blocks
    below = (owner[:, None] == owner[None, :]) & (own[None, :] < own[:, None])
    rank = jnp.sum(below.astype(jnp.int32), axis=1) // 2
    return send, owner * per_owner + rank


def steps(count, body):
    if count <= 16:
        for i in range(count):
            body(i)
    else:
        def step(i, carry):
            body(i)
            return carry
        lax.fori_loop(0, count, step, 0)


def kernel(
    domains, per_owner,
    send_ref, link_ref, src_ref, w_hbm, out_ref, rate_ref,
    w_ref, pack, buf, stage, land,
    w_sem, send_sem, recv_sem, fsend_sem, frecv_sem, osend_sem, orecv_sem,
):
    me = lax.axis_index("dom")
    core = lax.axis_index("tm")
    other = 1 - core
    tiles, link_count = w_ref.shape[0], w_ref.shape[1]
    mesh_type = pl.DeviceIdType.MESH

    def offset(i):
        return domains // 2 + ((i + 1) // 2) * (1 - 2 * (i % 2))

    barrier = pltpu.get_barrier_semaphore()

    def greet(i):
        to = lax.rem(me + i + 1, domains)
        pl.semaphore_signal(barrier, inc=1, device_id=(to, core), device_id_type=mesh_type)

    steps(domains - 1, greet)
    pl.semaphore_signal(barrier, inc=1, device_id=(me, other), device_id_type=mesh_type)

    loads = [pltpu.make_async_copy(w_hbm.at[t], w_ref.at[t], w_sem.at[t]) for t in range(tiles)]
    for load in loads:
        load.start()

    def fill(d):
        for j in range(per_owner):
            pack[d, j] = src_ref[send_ref[d * per_owner + j]]

    steps(domains, fill)
    for j in range(per_owner):
        buf[core, me * per_owner + j] = src_ref[send_ref[me * per_owner + j]]

    pl.semaphore_wait(barrier, domains)

    def exchange(to, frm):
        return pltpu.make_async_remote_copy(
            src_ref=pack.at[to],
            dst_ref=buf.at[core, pl.ds(frm * per_owner, per_owner)],
            send_sem=send_sem.at[to],
            recv_sem=recv_sem.at[frm],
            device_id=(to, core),
            device_id_type=mesh_type,
        )

    def send(i):
        exchange(lax.rem(me + offset(i), domains), me).start()

    steps(domains - 1, send)

    def forward(source, frm):
        return pltpu.make_async_remote_copy(
            src_ref=source,
            dst_ref=buf.at[core, pl.ds(frm * per_owner, per_owner)],
            send_sem=fsend_sem.at[frm],
            recv_sem=frecv_sem.at[frm],
            device_id=(me, other),
            device_id_type=mesh_type,
        )

    def landed(frm):
        return pltpu.make_async_remote_copy(
            src_ref=pack.at[0],
            dst_ref=buf.at[other, pl.ds(frm * per_owner, per_owner)],
            send_sem=fsend_sem.at[frm],
            recv_sem=frecv_sem.at[frm],
            device_id=(me, other),
            device_id_type=mesh_type,
        )

    forward(pack.at[me], me).start()

    def arrive(i):
        frm = lax.rem(me - offset(i) + domains, domains)
        incoming = pltpu.make_async_remote_copy(
            src_ref=pack.at[0],
            dst_ref=buf.at[core, pl.ds(frm * per_owner, per_owner)],
            send_sem=send_sem.at[frm],
            recv_sem=recv_sem.at[frm],
            device_id=(frm, core),
            device_id_type=mesh_type,
        )
        incoming.wait_recv()
        forward(buf.at[core, pl.ds(frm * per_owner, per_owner)], frm).start()

    steps(domains - 1, arrive)
    steps(domains, lambda d: landed(d).wait_recv())
    for load in loads:
        load.wait()

    swaps = []
    comps, half = src_ref.shape[1], src_ref.shape[2]
    span = 2 * half
    count = comps * span
    width = w_ref.shape[3]
    sample = lax.rem(lax.broadcasted_iota(jnp.int32, (count, width), 0), span)
    mine = pl.ds(pl.multiple_of(core * width, width), width)
    theirs = pl.ds(pl.multiple_of(other * width, width), width)
    for t in range(tiles):
        total = jnp.zeros((count, width), jnp.float32)
        for k in range(link_count):
            slot = link_ref[t * link_count + k]
            early = buf[0, slot].astype(jnp.float32)
            late = buf[1, slot].astype(jnp.float32)
            parts = []
            for p in range(comps):
                parts += [early[p], late[p]]
            lhs = jnp.concatenate(parts, axis=0).astype(jnp.bfloat16)
            total += jnp.dot(lhs, w_ref[t, k], preferred_element_type=jnp.float32)
        later = pltpu.roll(total, count - 1, 0)
        prior = pltpu.roll(total, 1, 0)
        rate = jnp.where(
            sample == 0,
            later - total,
            jnp.where(sample == span - 1, total - prior, (later - prior) * 0.5),
        )
        for which, value, target in ((0, total, out_ref), (1, rate, rate_ref)):
            value = value.reshape(comps, 2, half, width)
            lower, upper = value[:, 0], value[:, 1]
            target[t, :, :, mine] = jnp.where(core == 0, lower, upper).astype(jnp.bfloat16)
            stage[t, which] = jnp.where(core == 0, upper, lower).astype(jnp.bfloat16)
        swap = pltpu.make_async_remote_copy(
            src_ref=stage.at[t],
            dst_ref=land.at[t],
            send_sem=osend_sem.at[t],
            recv_sem=orecv_sem.at[t],
            device_id=(me, other),
            device_id_type=mesh_type,
        )
        swap.start()
        swaps.append(swap)

    def drain(i):
        exchange(lax.rem(me + i + 1, domains), me).wait_send()

    steps(domains - 1, drain)
    steps(domains, lambda d: forward(buf.at[core, pl.ds(0, per_owner)], d).wait_send())
    for t in range(tiles):
        swaps[t].wait()
        out_ref[t, :, :, theirs] = land[t, 0]
        rate_ref[t, :, :, theirs] = land[t, 1]


def shards(sources, weights, intersect, block_row, slot_tile):
    domains = lax.axis_size("dom")
    tiles, link_count, cells, width = weights.shape
    blocks, comps, half, _ = sources.shape
    pool = tiles * link_count // 2
    per_owner = (pool + domains - 1) // domains
    send, link = tables(
        sources, weights, intersect, block_row, slot_tile, per_owner, domains
    )
    vmem, smem = pltpu.VMEM, pltpu.SMEM
    out = jax.ShapeDtypeStruct((tiles, comps, half, 2 * width), jnp.bfloat16)
    block = (comps, half, cells)
    dma = pltpu.SemaphoreType.DMA
    return pl.pallas_call(
        functools.partial(kernel, domains, per_owner),
        out_shape=(out, out),
        in_specs=[
            pl.BlockSpec(memory_space=smem),
            pl.BlockSpec(memory_space=smem),
            pl.BlockSpec(memory_space=vmem),
            pl.BlockSpec(memory_space=pl.ANY),
        ],
        out_specs=(pl.BlockSpec(memory_space=vmem),) * 2,
        scratch_shapes=[
            vmem((tiles, link_count, cells, width), jnp.bfloat16),
            vmem((domains, per_owner) + block, jnp.bfloat16),
            vmem((2, domains * per_owner) + block, jnp.bfloat16),
            vmem((tiles, 2, comps, half, width), jnp.bfloat16),
            vmem((tiles, 2, comps, half, width), jnp.bfloat16),
            dma((tiles,)),
            dma((domains,)),
            dma((domains,)),
            dma((domains,)),
            dma((domains,)),
            dma((tiles,)),
            dma((tiles,)),
        ],
        compiler_params=pltpu.CompilerParams(collective_id=0, has_side_effects=True),
        cost_estimate=pl.CostEstimate(
            flops=4 * comps * half * weights.size, bytes_accessed=2 * weights.size, transcendentals=0
        ),
    )(send, link, sources, weights)


def solution(mesh):
    return jax.shard_map(
        shards,
        mesh=mesh,
        in_specs=(P("dom", None, "tm", None), P("dom", None, None, "tm"), P(), P(), P()),
        out_specs=(P("dom", None, "tm", None), P("dom", None, "tm", None)),
        check_vma=False,
    )
```

time: 56.6 us -> 30.4 us (0.54)
  Pallas kernels: 0 us -> 21.3 us
  between operations: 14.3 us -> 0.67 us
  waiting for transfers between devices: 12.4 us -> 0 us
  starting transfers between devices: 11 us -> 0 us
  local copies, waits for them, and re-layouts: 10.7 us -> 3.53 us
  matrix products: 3.78 us -> 0 us
    pallas_call x0 -> x1, Pallas kernels: none -> 21.3 us  [shards(): pl.pallas_call(functools.partial(kernel, domains, per_owner), out_shape=(...]
    all_to_all x1 -> x0, waiting for transfers between devices: 9.96 us -> none  [shards(): lax.all_to_all(packed, 'dom', split_axis=0, concat_axis=0, tiled=True)]
    all_to_all x1 -> x0, starting transfers between devices: 8.34 us -> none  [shards(): lax.all_to_all(packed, 'dom', split_axis=0, concat_axis=0, tiled=True)]
    gather x8 -> x0, local copies, waits for them, and re-layouts: 7.77 us -> none  [the longest x2 5.06 us: shards(): jnp.take(block_row, jnp.take(intersect, slot_tile, axis=0), axis=0)]
    dot_general x1 -> x0, matrix products: 3.78 us -> none  [interpolate(): jnp.einsum('tkrc,tkcn->trn', picked, used_weights, preferred_element_type...]
    reduce_sum x0 -> x3, other arithmetic: none -> 2.94 us  [the longest x1 1.59 us: tables(): jnp.sum(jnp.where(slot_tile[:, None, None] == tile_ids[None, :, None], in...]
    ppermute x2 -> x0, starting transfers between devices: 2.58 us -> none  [the longest x1 1.29 us: with_halo(): lax.ppermute(head, axis, [((i + 1) % count, i) for i in range(ends)])]
    unnamed x8 -> x2, local copies, waits for them, and re-layouts: 0.81 us -> 2.77 us
  transfers between devices with their start and end apart: 4 -> 0, of which waited for: 2 -> 0; matrix products, arithmetic and copies ran while one was open for 25% -> 0% of each run, Pallas kernels for 0% -> 0%
where the time goes in v1:
time: 30.4 us; the launch traced here: 30 us
  Pallas kernels  21.3 us (70%)
  other arithmetic  4.55 us (15%)
  local copies, waits for them, and re-layouts  3.53 us (12%)
  between operations  0.67 us (2%)
    pallas_call x1, Pallas kernels, shards(): pl.pallas_call(functools.partial(kernel, domains, per_owner), out_shape=(...  21.3 us
    unnamed x2, local copies, waits for them, and re-layouts  2.77 us
    reduce_sum x1, other arithmetic, tables(): jnp.sum(jnp.where(slot_tile[:, None, None] == tile_ids[None, :, None], in...  1.59 us
    reduce_sum x1, other arithmetic, tables(): jnp.sum(jnp.where(named[:, :, None] == block_ids, block_row, 0), axis=2)  1.17 us
    eq x1, other arithmetic, tables(): slot_tile[:, None, None] == tile_ids[None, :, None]  0.73 us

profile of v1, /device:TPU:0, one launch (start us, length us, event | category | flops | bytes accessed | tf_op | source)
XLA Modules:
  0.0 30.0 jit_solution(9231393849538014599)
XLA Ops:
  0.6 0.7 %iota_compare_fusion.1 = pred[48,48]{1,0:T(8,128)(4,1)S(1)} fusion(s32[48]{0:T(128)} %param.9), kind=kLoop, calls=%fused_computation.4 | loop fusion | flops 2304 | bytes 2496 | tf_op jit(solution)/shard_map/eq | solution.py:17
  1.4 1.6 %select_reduce_fusion.1 = s32[48,16]{1,0:T(8,128)S(1)} fusion(s32[48,16]{0,1:T(8,128)} %param.7, pred[48,48]{1,0:T(8,128)(4,1)S(1)} %iota_compare_fusion.1), kind=kLoop, calls=%fused_computation.2 | loop fusion | flops 72960 | bytes 8448 | tf_op jit(solution)/shard_map/reduce_sum | solution.py:16
  3.0 0.1 eq.51
  3.0 1.2 %select_reduce_fusion = s32[16,48]{1,0:T(8,128)S(1)} fusion(s32[256]{0:T(256)} %param.8, s32[16,48]{1,0:T(8,128)S(1)} %eq.51), kind=kLoop, calls=%fused_computation | loop fusion | flops 589056 | bytes 7168 | tf_op jit(solution)/shard_map/reduce_sum | solution.py:21
  4.2 0.1 select_reduce_fusion.3
  4.3 0.2 select_reduce_fusion.2
  4.6 0.2 convert_reduce_fusion
  4.8 0.5 %fusion.link_ref = s32[48]{0:T(128)} fusion(s32[48]{0:T(128)S(1)} %convert_reduce_fusion, s32[48]{0:T(128)S(1)} %get-tuple-element.2), kind=kLoop, calls=%fused_computation.21 | loop fusion | flops 816 | bytes 576 | tf_op jit(solution)/shard_map/add | solution.py:36
  5.3 0.1 copy.11
  5.4 0.6 %reshape.65.send_ref = s32[32]{0:T(128)} reshape(s32[16,2]{1,0:T(8,128)S(1)} %copy.11) | data formatting | bytes 256 | tf_op jit(solution)/shard_map/reshape | solution.py:31
  6.0 21.3 %shard_map.68 = (bf16[3,3,8,256]{3,2,1,0:T(8,128)(2,1)}, bf16[3,3,8,256]{3,2,1,0:T(8,128)(2,1)}) custom-call(s32[32]{0:T(128)} %reshape.65.send_ref, s32[48]{0:T(128)} %fusion.link_ref, bf16[16,3,8,256]{3,2,1,0:T(8,128)(2,1)} %src_ref.1, bf16[3,16,256,128]{3,2,1,0:T(8,128)(2,1)} %w_hbm.1), custom_call_target="tpu_custom_call" | custom-call | flops 150994944 | bytes 3145728 | tf_op jit(solution)/shard_map/pallas_call | solution.py:209
  27.3 1.4 %copy.14 = bf16[3,3,8,256]{3,2,1,0:T(8,128)(2,1)} copy(bf16[3,3,8,256]{3,2,1,0:T(8,128)(2,1)} %get-tuple-element.6) | data formatting | bytes 73728
  28.6 1.4 %copy.15 = bf16[3,3,8,256]{3,2,1,0:T(8,128)(2,1)} copy(bf16[3,3,8,256]{3,2,1,0:T(8,128)(2,1)} %get-tuple-element.7) | data formatting | bytes 73728
  (3 shorter events, 0.0 us)

commit v2 on v1

v2 whole, which is shorter than its diff:
```python
import functools

import jax
import jax.numpy as jnp
from jax import lax
from jax.experimental import pallas as pl
from jax.experimental.pallas import tpu as pltpu
from jax.sharding import PartitionSpec as P


BIG = 1 << 30


def lookup(table, index):
    lanes = 128
    within, group = index & (lanes - 1), index >> 7
    outs = []
    for at in range(0, index.shape[1], lanes):
        value = jnp.zeros((index.shape[0], lanes), jnp.int32)
        for g in range(table.shape[1] // lanes):
            got = jnp.take_along_axis(
                table[:, g * lanes : (g + 1) * lanes],
                within[:, at : at + lanes],
                axis=1,
                mode="promise_in_bounds",
            )
            value = jnp.where(group[:, at : at + lanes] == g, got, value)
        outs.append(value)
    return outs[0] if len(outs) == 1 else jnp.concatenate(outs, axis=1)


def steps(count, body):
    if count <= 16:
        for i in range(count):
            body(i)
    else:
        def step(i, carry):
            body(i)
            return carry
        lax.fori_loop(0, count, step, 0)


def kernel(
    domains, per_owner,
    tile_ref, row_ref, cross_ref, src_ref, w_hbm, out_ref,
    wide_tile, wide_row, wide_cross, send_to, link_one, link_two,
    w_ref, pack, buf, acc, stage, land,
    w_sem, send_sem, recv_sem, fsend_sem, frecv_sem, osend_sem, orecv_sem,
):
    me = lax.axis_index("dom")
    core = lax.axis_index("tm")
    other = 1 - core
    links, width = w_ref.shape[0], w_ref.shape[2]
    blocks, comps, half, cells = src_ref.shape
    tiles = acc.shape[0]
    link_count = links // tiles
    span = 2 * half
    count = comps * span
    mesh_type = pl.DeviceIdType.MESH

    def offset(i):
        return domains // 2 + ((i + 1) // 2) * (1 - 2 * (i % 2))

    barrier = pltpu.get_barrier_semaphore()

    def greet(i):
        to = lax.rem(me + i + 1, domains)
        pl.semaphore_signal(barrier, inc=1, device_id=(to, core), device_id_type=mesh_type)

    steps(domains - 1, greet)
    pl.semaphore_signal(barrier, inc=1, device_id=(me, other), device_id_type=mesh_type)

    loads = [
        pltpu.make_async_copy(
            w_hbm.at[pl.ds(t * link_count, link_count)],
            w_ref.at[pl.ds(t * link_count, link_count)],
            w_sem.at[t],
        )
        for t in range(tiles)
    ]
    for load in loads:
        load.start()

    wide_tile[...] = jnp.zeros_like(wide_tile)
    wide_cross[...] = jnp.zeros_like(wide_cross)
    wide_row[...] = jnp.zeros_like(wide_row)
    wide_tile[:, : tile_ref.shape[1]] = jnp.broadcast_to(
        tile_ref[...], (link_count, tile_ref.shape[1])
    )
    wide_cross[:, : cross_ref.shape[1]] = cross_ref[...]
    wide_row[:, : row_ref.shape[1]] = jnp.broadcast_to(
        row_ref[...], (link_count, row_ref.shape[1])
    )
    rows = lookup(wide_row[...], lookup(wide_cross[...], wide_tile[...]))

    slots = rows.shape[1]
    lane = lax.broadcasted_iota(jnp.int32, (1, slots), 1)
    place = lax.rem(lane, tiles)
    local = rows - me * blocks
    mine = (local >= 0) & (local < blocks)
    last = jnp.full((1, slots), -1, jnp.int32)
    for j in range(per_owner):
        least = jnp.min(jnp.where(mine & (local > last), local, BIG), axis=0, keepdims=True)
        joint = least
        for t in range(1, tiles):
            joint = jnp.minimum(joint, pltpu.roll(least, slots - t, 1))
        last = joint
        for t in range(1, tiles):
            last = jnp.where(place == t, pltpu.roll(joint, t, 1), last)
        index = jnp.minimum(last, blocks - 1)
        for d in range(domains):
            send_to[d * per_owner + j] = index[0, d * tiles]

    def fill(d):
        for j in range(per_owner):
            pack[d, j] = src_ref[send_to[d * per_owner + j]]

    steps(domains, fill)
    for j in range(per_owner):
        buf[core, me * per_owner + j] = src_ref[send_to[me * per_owner + j]]

    pl.semaphore_wait(barrier, domains)

    def exchange(to, frm):
        return pltpu.make_async_remote_copy(
            src_ref=pack.at[to],
            dst_ref=buf.at[core, pl.ds(frm * per_owner, per_owner)],
            send_sem=send_sem.at[to],
            recv_sem=recv_sem.at[frm],
            device_id=(to, core),
            device_id_type=mesh_type,
        )

    def send(i):
        exchange(lax.rem(me + offset(i), domains), me).start()

    steps(domains - 1, send)

    def forward(source, frm):
        return pltpu.make_async_remote_copy(
            src_ref=source,
            dst_ref=buf.at[core, pl.ds(frm * per_owner, per_owner)],
            send_sem=fsend_sem.at[frm],
            recv_sem=frecv_sem.at[frm],
            device_id=(me, other),
            device_id_type=mesh_type,
        )

    def landed(frm):
        return pltpu.make_async_remote_copy(
            src_ref=pack.at[0],
            dst_ref=buf.at[other, pl.ds(frm * per_owner, per_owner)],
            send_sem=fsend_sem.at[frm],
            recv_sem=frecv_sem.at[frm],
            device_id=(me, other),
            device_id_type=mesh_type,
        )

    forward(pack.at[me], me).start()

    owners = -(-domains // 128) * 128
    around = lax.broadcasted_iota(jnp.int32, (1, owners), 1)
    owner = around + me
    owner = jnp.where(owner >= domains, owner - domains, owner)
    link = lax.broadcasted_iota(jnp.int32, (link_count, owners), 0)
    locals_ = []
    for t in range(tiles):
        column = jnp.sum(jnp.where(lane == me * tiles + t, rows, 0), axis=1, keepdims=True)
        at = column - owner * blocks
        locals_.append(jnp.where((at >= 0) & (at < blocks), at, BIG))
    last = jnp.full((1, owners), -1, jnp.int32)
    for j in range(per_owner):
        least = [jnp.where(at > last, at, BIG) for at in locals_]
        last = jnp.min(functools.reduce(jnp.minimum, least), axis=0, keepdims=True)
        one = jnp.full((link_count, owners), BIG, jnp.int32)
        two = jnp.full((link_count, owners), -1, jnp.int32)
        for t in range(tiles):
            hit = (locals_[t] == last) & (last < BIG)
            one = jnp.minimum(one, jnp.where(hit, link + t * link_count, BIG))
            two = jnp.maximum(two, jnp.where(hit, link + t * link_count, -1))
        one = jnp.min(one, axis=0, keepdims=True)
        two = jnp.max(two, axis=0, keepdims=True)
        for i in range(domains):
            link_one[i * per_owner + j] = one[0, i]
            link_two[i * per_owner + j] = two[0, i]

    acc[...] = jnp.zeros_like(acc)
    for load in loads:
        load.wait()

    def product(i):
        frm = lax.rem(me + i, domains)
        landed(frm).wait_recv()
        for j in range(per_owner):
            early = buf[0, frm * per_owner + j].astype(jnp.float32)
            late = buf[1, frm * per_owner + j].astype(jnp.float32)
            parts = []
            for p in range(comps):
                parts += [early[p], late[p]]
            lhs = jnp.concatenate(parts, axis=0).astype(jnp.bfloat16)
            one = link_one[i * per_owner + j]
            two = link_two[i * per_owner + j]
            pair = jnp.concatenate(
                [w_ref[jnp.minimum(one, links - 1)], w_ref[jnp.maximum(two, 0)]], axis=1
            )
            both = jnp.dot(lhs, pair, preferred_element_type=jnp.float32)
            for t in range(tiles):
                first, end = t * link_count, (t + 1) * link_count
                acc[t] += jnp.where((one >= first) & (one < end), both[:, :width], 0.0) + jnp.where(
                    (two >= first) & (two < end), both[:, width:], 0.0
                )

    def arrive(i):
        frm = lax.rem(me - offset(i) + domains, domains)
        incoming = pltpu.make_async_remote_copy(
            src_ref=pack.at[0],
            dst_ref=buf.at[core, pl.ds(frm * per_owner, per_owner)],
            send_sem=send_sem.at[frm],
            recv_sem=recv_sem.at[frm],
            device_id=(frm, core),
            device_id_type=mesh_type,
        )
        incoming.wait_recv()
        forward(buf.at[core, pl.ds(frm * per_owner, per_owner)], frm).start()

    lag = 2

    def both_steps(i):
        if isinstance(i, int):
            if i < domains - 1:
                arrive(i)
            if i == 0:
                product(0)
            if i >= lag:
                product(domains - offset(i - lag))

    if domains <= 16:
        for i in range(domains - 1 + lag):
            both_steps(i)
    else:
        steps(domains - 1, arrive)
        steps(domains, product)

    sample = lax.rem(lax.broadcasted_iota(jnp.int32, (count, width), 0), span)
    mine = pl.ds(pl.multiple_of(core * width, width), width)
    theirs = pl.ds(pl.multiple_of(other * width, width), width)
    swaps = []
    for t in range(tiles):
        total = acc[t]
        later = pltpu.roll(total, count - 1, 0)
        prior = pltpu.roll(total, 1, 0)
        rate = jnp.where(
            sample == 0,
            later - total,
            jnp.where(sample == span - 1, total - prior, (later - prior) * 0.5),
        )
        for which, value in ((0, total), (1, rate)):
            value = value.reshape(comps, 2, half, width)
            lower, upper = value[:, 0], value[:, 1]
            out_ref[which, t, :, :, mine] = jnp.where(core == 0, lower, upper).astype(jnp.bfloat16)
            stage[t, which] = jnp.where(core == 0, upper, lower).astype(jnp.bfloat16)
    for t in range(tiles):
        swap = pltpu.make_async_remote_copy(
            src_ref=stage.at[t],
            dst_ref=land.at[t],
            send_sem=osend_sem.at[t],
            recv_sem=orecv_sem.at[t],
            device_id=(me, other),
            device_id_type=mesh_type,
        )
        swap.start()
        swaps.append(swap)

    def drain(i):
        exchange(lax.rem(me + i + 1, domains), me).wait_send()

    steps(domains - 1, drain)
    steps(domains, lambda d: forward(buf.at[core, pl.ds(0, per_owner)], d).wait_send())
    for t in range(tiles):
        swaps[t].wait()
        for which in range(2):
            out_ref[which, t, :, :, theirs] = land[t, which]


def deliver(both_ref, source_ref, rate_ref):
    source_ref[...] = both_ref[0]
    rate_ref[...] = both_ref[1]


def shards(sources, weights, intersect, block_row, slot_tile):
    domains = lax.axis_size("dom")
    tiles, link_count, cells, width = weights.shape
    blocks, comps, half, _ = sources.shape
    links = tiles * link_count
    pool = links // 2
    per_owner = (pool + domains - 1) // domains
    vmem, smem = pltpu.VMEM, pltpu.SMEM
    shape = (tiles, comps, half, 2 * width)
    out = jax.ShapeDtypeStruct(shape, jnp.bfloat16)
    block = (comps, half, cells)
    dma = pltpu.SemaphoreType.DMA
    in_vmem = pl.BlockSpec(memory_space=vmem)

    def wide(n):
        return vmem((link_count, -(-n // 128) * 128), jnp.int32)

    both = pl.pallas_call(
        functools.partial(kernel, domains, per_owner),
        out_shape=jax.ShapeDtypeStruct((2,) + shape, jnp.bfloat16),
        in_specs=[in_vmem, in_vmem, in_vmem, in_vmem, pl.BlockSpec(memory_space=pl.ANY)],
        out_specs=in_vmem,
        scratch_shapes=[
            wide(slot_tile.shape[0]),
            wide(block_row.shape[0]),
            wide(intersect.shape[0]),
            smem((domains * per_owner,), jnp.int32),
            smem((domains * per_owner,), jnp.int32),
            smem((domains * per_owner,), jnp.int32),
            vmem((links, cells, width), jnp.bfloat16),
            vmem((domains, per_owner) + block, jnp.bfloat16),
            vmem((2, domains * per_owner) + block, jnp.bfloat16),
            vmem((tiles, 2 * comps * half, width), jnp.float32),
            vmem((tiles, 2, comps, half, width), jnp.bfloat16),
            vmem((tiles, 2, comps, half, width), jnp.bfloat16),
            dma((tiles,)),
            dma((domains,)),
            dma((domains,)),
            dma((domains,)),
            dma((domains,)),
            dma((tiles,)),
            dma((tiles,)),
        ],
        compiler_params=pltpu.CompilerParams(collective_id=0, has_side_effects=True),
        cost_estimate=pl.CostEstimate(
            flops=4 * comps * half * weights.size,
            bytes_accessed=2 * weights.size,
            transcendentals=0,
        ),
    )(
        slot_tile.reshape(1, -1),
        block_row.reshape(1, -1),
        intersect.T,
        sources,
        weights.reshape(links, cells, width),
    )
    return pl.pallas_call(
        deliver,
        out_shape=(out, out),
        in_specs=[in_vmem],
        out_specs=(in_vmem, in_vmem),
    )(both)


def solution(mesh):
    return jax.shard_map(
        shards,
        mesh=mesh,
        in_specs=(P("dom", None, "tm", None), P("dom", None, None, "tm"), P(), P(), P()),
        out_specs=(P("dom", None, "tm", None), P("dom", None, "tm", None)),
        check_vma=False,
    )
```

time: 30.4 us -> 26 us (0.86)
  other arithmetic: 4.55 us -> 0 us
  Pallas kernels: 21.3 us -> 25.1 us
  local copies, waits for them, and re-layouts: 3.53 us -> 0 us
    pallas_call x1 -> x2, Pallas kernels: 21.3 us -> 25.1 us  [the longest x1 23.6 us: shards(): pl.pallas_call(functools.partial(kernel, domains, per_owner), out_shape=j...]
    reduce_sum x3 -> x0, other arithmetic: 2.94 us -> none  [the longest x1 1.59 us: tables(): jnp.sum(jnp.where(slot_tile[:, None, None] == tile_ids[None, :, None], in...]
    unnamed x2 -> x0, local copies, waits for them, and re-layouts: 2.77 us -> none
    eq x2 -> x0, other arithmetic: 0.75 us -> none  [the longest x1 0.73 us: tables(): slot_tile[:, None, None] == tile_ids[None, :, None]]
    reshape x1 -> x0, local copies, waits for them, and re-layouts: 0.6 us -> none  [tables(): send = jnp.concatenate(picks, axis=1).reshape(-1)]
    add x1 -> x0, other arithmetic: 0.53 us -> none  [tables(): return (send, owner * per_owner + rank)]
    reduce_min x2 -> x0, other arithmetic: 0.31 us -> none  [tables(): last = jnp.min(ahead, axis=1, keepdims=True)]
where the time goes in v2:
time: 26 us; the launch traced here: 25.8 us
  Pallas kernels  25.1 us (97%)
  between operations  0.64 us (2%)
    pallas_call x1, Pallas kernels, shards(): pl.pallas_call(functools.partial(kernel, domains, per_owner), out_shape=j...  23.6 us
    pallas_call x1, Pallas kernels, shards(): pl.pallas_call(deliver, out_shape=(out, out), in_specs=[in_vmem], out_spe...  1.52 us

profile of v2, /device:TPU:0, one launch (start us, length us, event | category | flops | bytes accessed | tf_op | source)
XLA Modules:
  0.0 25.8 jit_solution(16523121748472748128)
XLA Ops:
  0.6 23.6 %shard_map.68.both_ref = bf16[2,3,3,8,256]{4,3,2,1,0:T(8,128)(2,1)} custom-call(s32[1,48]{1,0:T(1,128)} %bitcast.7, s32[1,256]{1,0:T(1,128)} %bitcast.6, s32[16,48]{1,0:T(8,128)} %bitcast.5, bf16[16,3,8,256]{3,2,1,0:T(8,128)(2,1)} %src_ref.1, bf16[48,256,128]{2,1,0:T(8,128)(2,1)} %bitcast.4), custom_call_target="tpu_custom_call" | custom-call | flops 150994944 | bytes 3145728 | tf_op jit(solution)/shard_map/pallas_call | solution.py:307
  24.3 1.5 %shard_map.69 = (bf16[3,3,8,256]{3,2,1,0:T(8,128)(2,1)}, bf16[3,3,8,256]{3,2,1,0:T(8,128)(2,1)}) custom-call(bf16[2,3,3,8,256]{4,3,2,1,0:T(8,128)(2,1)} %shard_map.68.both_ref), custom_call_target="tpu_custom_call" | custom-call | tf_op jit(solution)/shard_map/pallas_call | solution.py:346

commit v3 on v2

--- a/solution.py
+++ b/solution.py
@@ -42,20 +42,20 @@
 
 def kernel(
     domains, per_owner,
-    tile_ref, row_ref, cross_ref, src_ref, w_hbm, out_ref,
+    tile_hbm, row_hbm, cross_hbm, src_hbm, w_hbm, out_ref,
+    tile_ref, row_ref, cross_ref, src_ref,
     wide_tile, wide_row, wide_cross, send_to, link_one, link_two,
-    w_ref, pack, buf, acc, stage, land,
-    w_sem, send_sem, recv_sem, fsend_sem, frecv_sem, osend_sem, orecv_sem,
+    w_ref, pack, buf, acc, edge, beyond,
+    in_sem, w_sem, send_sem, recv_sem, wsend_sem, wrecv_sem, edge_sem,
 ):
     me = lax.axis_index("dom")
     core = lax.axis_index("tm")
     other = 1 - core
-    links, width = w_ref.shape[0], w_ref.shape[2]
+    links, width = w_ref.shape[1], w_ref.shape[3]
     blocks, comps, half, cells = src_ref.shape
     tiles = acc.shape[0]
     link_count = links // tiles
-    span = 2 * half
-    count = comps * span
+    count = comps * half
     mesh_type = pl.DeviceIdType.MESH
 
     def offset(i):
@@ -70,13 +70,23 @@
     steps(domains - 1, greet)
     pl.semaphore_signal(barrier, inc=1, device_id=(me, other), device_id_type=mesh_type)
 
+    inputs = [
+        pltpu.make_async_copy(source, target, in_sem.at[i])
+        for i, (source, target) in enumerate(
+            (
+                (cross_hbm, cross_ref),
+                (tile_hbm, tile_ref),
+                (row_hbm, row_ref),
+                (src_hbm, src_ref),
+            )
+        )
+    ]
+    for load in inputs:
+        load.start()
+    parts = [pl.ds(t * link_count, link_count) for t in range(tiles)]
     loads = [
-        pltpu.make_async_copy(
-            w_hbm.at[pl.ds(t * link_count, link_count)],
-            w_ref.at[pl.ds(t * link_count, link_count)],
-            w_sem.at[t],
-        )
-        for t in range(tiles)
+        pltpu.make_async_copy(w_hbm.at[part], w_ref.at[core, part], w_sem.at[t])
+        for t, part in enumerate(parts)
     ]
     for load in loads:
         load.start()
@@ -84,6 +94,8 @@
     wide_tile[...] = jnp.zeros_like(wide_tile)
     wide_cross[...] = jnp.zeros_like(wide_cross)
     wide_row[...] = jnp.zeros_like(wide_row)
+    for load in inputs[:3]:
+        load.wait()
     wide_tile[:, : tile_ref.shape[1]] = jnp.broadcast_to(
         tile_ref[...], (link_count, tile_ref.shape[1])
     )
@@ -115,16 +127,17 @@
         for j in range(per_owner):
             pack[d, j] = src_ref[send_to[d * per_owner + j]]
 
+    inputs[3].wait()
     steps(domains, fill)
     for j in range(per_owner):
-        buf[core, me * per_owner + j] = src_ref[send_to[me * per_owner + j]]
+        buf[me * per_owner + j] = src_ref[send_to[me * per_owner + j]]
 
     pl.semaphore_wait(barrier, domains)
 
     def exchange(to, frm):
         return pltpu.make_async_remote_copy(
             src_ref=pack.at[to],
-            dst_ref=buf.at[core, pl.ds(frm * per_owner, per_owner)],
+            dst_ref=buf.at[pl.ds(frm * per_owner, per_owner)],
             send_sem=send_sem.at[to],
             recv_sem=recv_sem.at[frm],
             device_id=(to, core),
@@ -136,27 +149,19 @@
 
     steps(domains - 1, send)
 
-    def forward(source, frm):
-        return pltpu.make_async_remote_copy(
-            src_ref=source,
-            dst_ref=buf.at[core, pl.ds(frm * per_owner, per_owner)],
-            send_sem=fsend_sem.at[frm],
-            recv_sem=frecv_sem.at[frm],
+    swaps = [
+        pltpu.make_async_remote_copy(
+            src_ref=w_hbm.at[part],
+            dst_ref=w_ref.at[core, part],
+            send_sem=wsend_sem.at[t],
+            recv_sem=wrecv_sem.at[t],
             device_id=(me, other),
             device_id_type=mesh_type,
         )
-
-    def landed(frm):
-        return pltpu.make_async_remote_copy(
-            src_ref=pack.at[0],
-            dst_ref=buf.at[other, pl.ds(frm * per_owner, per_owner)],
-            send_sem=fsend_sem.at[frm],
-            recv_sem=frecv_sem.at[frm],
-            device_id=(me, other),
-            device_id_type=mesh_type,
-        )
-
-    forward(pack.at[me], me).start()
+        for t, part in enumerate(parts)
+    ]
+    for swap in swaps:
+        swap.start()
 
     owners = -(-domains // 128) * 128
     around = lax.broadcasted_iota(jnp.int32, (1, owners), 1)
@@ -185,101 +190,96 @@
             link_two[i * per_owner + j] = two[0, i]
 
     acc[...] = jnp.zeros_like(acc)
-    for load in loads:
-        load.wait()
-
     def product(i):
         frm = lax.rem(me + i, domains)
-        landed(frm).wait_recv()
         for j in range(per_owner):
-            early = buf[0, frm * per_owner + j].astype(jnp.float32)
-            late = buf[1, frm * per_owner + j].astype(jnp.float32)
-            parts = []
-            for p in range(comps):
-                parts += [early[p], late[p]]
-            lhs = jnp.concatenate(parts, axis=0).astype(jnp.bfloat16)
+            rows_here = buf[frm * per_owner + j].astype(jnp.float32)
+            lhs = rows_here.reshape(count, cells).astype(jnp.bfloat16)
             one = link_one[i * per_owner + j]
             two = link_two[i * per_owner + j]
-            pair = jnp.concatenate(
-                [w_ref[jnp.minimum(one, links - 1)], w_ref[jnp.maximum(two, 0)]], axis=1
+            at_one, at_two = jnp.minimum(one, links - 1), jnp.maximum(two, 0)
+            quad = jnp.concatenate(
+                [w_ref[0, at_one], w_ref[1, at_one], w_ref[0, at_two], w_ref[1, at_two]], axis=1
             )
-            both = jnp.dot(lhs, pair, preferred_element_type=jnp.float32)
+            both = jnp.dot(lhs, quad, preferred_element_type=jnp.float32)
             for t in range(tiles):
                 first, end = t * link_count, (t + 1) * link_count
-                acc[t] += jnp.where((one >= first) & (one < end), both[:, :width], 0.0) + jnp.where(
-                    (two >= first) & (two < end), both[:, width:], 0.0
-                )
+                acc[t] += jnp.where(
+                    (one >= first) & (one < end), both[:, : 2 * width], 0.0
+                ) + jnp.where((two >= first) & (two < end), both[:, 2 * width :], 0.0)
 
     def arrive(i):
         frm = lax.rem(me - offset(i) + domains, domains)
         incoming = pltpu.make_async_remote_copy(
             src_ref=pack.at[0],
-            dst_ref=buf.at[core, pl.ds(frm * per_owner, per_owner)],
+            dst_ref=buf.at[pl.ds(frm * per_owner, per_owner)],
             send_sem=send_sem.at[frm],
             recv_sem=recv_sem.at[frm],
             device_id=(frm, core),
             device_id_type=mesh_type,
         )
         incoming.wait_recv()
-        forward(buf.at[core, pl.ds(frm * per_owner, per_owner)], frm).start()
-
-    lag = 2
-
-    def both_steps(i):
-        if isinstance(i, int):
-            if i < domains - 1:
-                arrive(i)
-            if i == 0:
-                product(0)
-            if i >= lag:
-                product(domains - offset(i - lag))
-
+
+    def weights_in():
+        for load in loads:
+            load.wait()
+        for t, part in enumerate(parts):
+            pltpu.make_async_remote_copy(
+                src_ref=w_hbm.at[part],
+                dst_ref=w_ref.at[other, part],
+                send_sem=wsend_sem.at[t],
+                recv_sem=wrecv_sem.at[t],
+                device_id=(me, other),
+                device_id_type=mesh_type,
+            ).wait_recv()
+
+    weights_in()
+    product(0)
     if domains <= 16:
-        for i in range(domains - 1 + lag):
-            both_steps(i)
+        for i in range(domains - 1):
+            arrive(i)
+            product(domains - offset(i))
     else:
         steps(domains - 1, arrive)
-        steps(domains, product)
-
-    sample = lax.rem(lax.broadcasted_iota(jnp.int32, (count, width), 0), span)
-    mine = pl.ds(pl.multiple_of(core * width, width), width)
-    theirs = pl.ds(pl.multiple_of(other * width, width), width)
-    swaps = []
-    for t in range(tiles):
-        total = acc[t]
-        later = pltpu.roll(total, count - 1, 0)
-        prior = pltpu.roll(total, 1, 0)
-        rate = jnp.where(
-            sample == 0,
-            later - total,
-            jnp.where(sample == span - 1, total - prior, (later - prior) * 0.5),
-        )
-        for which, value in ((0, total), (1, rate)):
-            value = value.reshape(comps, 2, half, width)
-            lower, upper = value[:, 0], value[:, 1]
-            out_ref[which, t, :, :, mine] = jnp.where(core == 0, lower, upper).astype(jnp.bfloat16)
-            stage[t, which] = jnp.where(core == 0, upper, lower).astype(jnp.bfloat16)
-    for t in range(tiles):
-        swap = pltpu.make_async_remote_copy(
-            src_ref=stage.at[t],
-            dst_ref=land.at[t],
-            send_sem=osend_sem.at[t],
-            recv_sem=orecv_sem.at[t],
-            device_id=(me, other),
-            device_id_type=mesh_type,
-        )
-        swap.start()
-        swaps.append(swap)
+        steps(domains - 1, lambda i: product(i + 1))
+
+    total = acc[...].reshape(tiles, comps, half, 2 * width)
+    edge[...] = jnp.where(core == 0, total[:, :, half - 1], total[:, :, 0])
+    halo = pltpu.make_async_remote_copy(
+        src_ref=edge,
+        dst_ref=beyond,
+        send_sem=edge_sem.at[0],
+        recv_sem=edge_sem.at[1],
+        device_id=(me, other),
+        device_id_type=mesh_type,
+    )
+    out_ref[0] = total.astype(jnp.bfloat16)
 
     def drain(i):
         exchange(lax.rem(me + i + 1, domains), me).wait_send()
 
     steps(domains - 1, drain)
-    steps(domains, lambda d: forward(buf.at[core, pl.ds(0, per_owner)], d).wait_send())
+    for swap in swaps:
+        swap.wait_send()
+    halo.start()
+    halo.wait()
+    sample = lax.broadcasted_iota(jnp.int32, (half, 2 * width), 0)
     for t in range(tiles):
-        swaps[t].wait()
-        for which in range(2):
-            out_ref[which, t, :, :, theirs] = land[t, which]
+        for p in range(comps):
+            here = total[t, p]
+            outer = jnp.broadcast_to(beyond[t, pl.ds(p, 1)], here.shape)
+            later = pltpu.roll(here, half - 1, 0)
+            prior = pltpu.roll(here, 1, 0)
+            later = jnp.where((sample == half - 1) & (core == 0), outer, later)
+            prior = jnp.where((sample == 0) & (core == 1), outer, prior)
+            rate = jnp.where(
+                (sample == 0) & (core == 0),
+                later - here,
+                jnp.where(
+                    (sample == half - 1) & (core == 1), here - prior, (later - prior) * 0.5
+                ),
+            )
+            out_ref[1, t, p] = rate.astype(jnp.bfloat16)
 
 
 def deliver(both_ref, source_ref, rate_ref):
@@ -307,28 +307,32 @@
     both = pl.pallas_call(
         functools.partial(kernel, domains, per_owner),
         out_shape=jax.ShapeDtypeStruct((2,) + shape, jnp.bfloat16),
-        in_specs=[in_vmem, in_vmem, in_vmem, in_vmem, pl.BlockSpec(memory_space=pl.ANY)],
+        in_specs=[pl.BlockSpec(memory_space=pl.ANY)] * 5,
         out_specs=in_vmem,
         scratch_shapes=[
+            vmem((1, slot_tile.shape[0]), jnp.int32),
+            vmem((1, block_row.shape[0]), jnp.int32),
+            vmem((link_count, intersect.shape[0]), jnp.int32),
+            vmem(sources.shape, jnp.bfloat16),
             wide(slot_tile.shape[0]),
             wide(block_row.shape[0]),
             wide(intersect.shape[0]),
             smem((domains * per_owner,), jnp.int32),
             smem((domains * per_owner,), jnp.int32),
             smem((domains * per_owner,), jnp.int32),
-            vmem((links, cells, width), jnp.bfloat16),
+            vmem((2, links, cells, width), jnp.bfloat16),
             vmem((domains, per_owner) + block, jnp.bfloat16),
-            vmem((2, domains * per_owner) + block, jnp.bfloat16),
-            vmem((tiles, 2 * comps * half, width), jnp.float32),
-            vmem((tiles, 2, comps, half, width), jnp.bfloat16),
-            vmem((tiles, 2, comps, half, width), jnp.bfloat16),
+            vmem((domains * per_owner,) + block, jnp.bfloat16),
+            vmem((tiles, comps * half, 2 * width), jnp.float32),
+            vmem((tiles, comps, 2 * width), jnp.float32),
+            vmem((tiles, comps, 2 * width), jnp.float32),
+            dma((4,)),
             dma((tiles,)),
-            dma((domains,)),
-            dma((domains,)),
             dma((domains,)),
             dma((domains,)),
             dma((tiles,)),
             dma((tiles,)),
+            dma((2,)),
         ],
         compiler_params=pltpu.CompilerParams(collective_id=0, has_side_effects=True),
         cost_estimate=pl.CostEstimate(

time: 26 us -> 22.8 us (0.88)
  Pallas kernels: 25.1 us -> 22 us
    pallas_call x1, Pallas kernels: 23.6 us -> 20.5 us  [shards(): pl.pallas_call(functools.partial(kernel, domains, per_owner), out_shape=j...]
where the time goes in v3:
time: 22.8 us; the launch traced here: 22.6 us
  Pallas kernels  22 us (96%)
  between operations  0.64 us (3%)
    pallas_call x1, Pallas kernels, shards(): pl.pallas_call(functools.partial(kernel, domains, per_owner), out_shape=j...  20.5 us
    pallas_call x1, Pallas kernels, shards(): pl.pallas_call(deliver, out_shape=(out, out), in_specs=[in_vmem], out_spe...  1.52 us

profile of v3, /device:TPU:0, one launch (start us, length us, event | category | flops | bytes accessed | tf_op | source)
XLA Modules:
  0.0 22.6 jit_solution(10309756895150906408)
XLA Ops:
  0.6 20.5 %shard_map.68.both_ref = bf16[2,3,3,8,256]{4,3,2,1,0:T(8,128)(2,1)} custom-call(s32[1,48]{1,0:T(1,128)} %bitcast.7, s32[1,256]{1,0:T(1,128)} %bitcast.6, s32[16,48]{1,0:T(8,128)} %bitcast.5, bf16[16,3,8,256]{3,2,1,0:T(8,128)(2,1)} %src_hbm.1, bf16[48,256,128]{2,1,0:T(8,128)(2,1)} %bitcast.4), custom_call_target="tpu_custom_call" | custom-call | flops 150994944 | bytes 3145728 | tf_op jit(solution)/shard_map/pallas_call | solution.py:307
  21.1 1.5 %shard_map.69 = (bf16[3,3,8,256]{3,2,1,0:T(8,128)(2,1)}, bf16[3,3,8,256]{3,2,1,0:T(8,128)(2,1)}) custom-call(bf16[2,3,3,8,256]{4,3,2,1,0:T(8,128)(2,1)} %shard_map.68.both_ref), custom_call_target="tpu_custom_call" | custom-call | tf_op jit(solution)/shard_map/pallas_call | solution.py:350

commit v4 on v3

--- a/solution.py
+++ b/solution.py
@@ -59,7 +59,7 @@
     mesh_type = pl.DeviceIdType.MESH
 
     def offset(i):
-        return domains // 2 + ((i + 1) // 2) * (1 - 2 * (i % 2))
+        return i + 1
 
     barrier = pltpu.get_barrier_semaphore()
 
@@ -151,7 +151,7 @@
 
     swaps = [
         pltpu.make_async_remote_copy(
-            src_ref=w_hbm.at[part],
+            src_ref=w_ref.at[core, part],
             dst_ref=w_ref.at[core, part],
             send_sem=wsend_sem.at[t],
             recv_sem=wrecv_sem.at[t],
@@ -160,7 +160,8 @@
         )
         for t, part in enumerate(parts)
     ]
-    for swap in swaps:
+    for load, swap in zip(loads, swaps):
+        load.wait()
         swap.start()
 
     owners = -(-domains // 128) * 128
@@ -221,8 +222,6 @@
         incoming.wait_recv()
 
     def weights_in():
-        for load in loads:
-            load.wait()
         for t, part in enumerate(parts):
             pltpu.make_async_remote_copy(
                 src_ref=w_hbm.at[part],

time: 22.8 us -> 20.2 us (0.89)
  Pallas kernels: 22 us -> 19.3 us
    pallas_call x1, Pallas kernels: 20.5 us -> 17.8 us  [shards(): pl.pallas_call(functools.partial(kernel, domains, per_owner), out_shape=j...]
where the time goes in v4:
time: 20.2 us; the launch traced here: 19.9 us
  Pallas kernels  19.3 us (96%)
  between operations  0.64 us (3%)
    pallas_call x1, Pallas kernels, shards(): pl.pallas_call(functools.partial(kernel, domains, per_owner), out_shape=j...  17.8 us
    pallas_call x1, Pallas kernels, shards(): pl.pallas_call(deliver, out_shape=(out, out), in_specs=[in_vmem], out_spe...  1.52 us

profile of v4, /device:TPU:0, one launch (start us, length us, event | category | flops | bytes accessed | tf_op | source)
XLA Modules:
  0.0 19.9 jit_solution(8449481517691092472)
XLA Ops:
  0.6 17.8 %shard_map.68.both_ref = bf16[2,3,3,8,256]{4,3,2,1,0:T(8,128)(2,1)} custom-call(s32[1,48]{1,0:T(1,128)} %bitcast.7, s32[1,256]{1,0:T(1,128)} %bitcast.6, s32[16,48]{1,0:T(8,128)} %bitcast.5, bf16[16,3,8,256]{3,2,1,0:T(8,128)(2,1)} %src_hbm.1, bf16[48,256,128]{2,1,0:T(8,128)(2,1)} %bitcast.4), custom_call_target="tpu_custom_call" | custom-call | flops 150994944 | bytes 3145728 | tf_op jit(solution)/shard_map/pallas_call | solution.py:306
  18.4 1.5 %shard_map.69 = (bf16[3,3,8,256]{3,2,1,0:T(8,128)(2,1)}, bf16[3,3,8,256]{3,2,1,0:T(8,128)(2,1)}) custom-call(bf16[2,3,3,8,256]{4,3,2,1,0:T(8,128)(2,1)} %shard_map.68.both_ref), custom_call_target="tpu_custom_call" | custom-call | tf_op jit(solution)/shard_map/pallas_call | solution.py:349
